TPU v7x, 256 devices: a whole 4x4x8 slice. The times are simulated.
256 devices in a mesh: dp: 8 (over x, core), expert: 32 (over y, z).
Axes of the slice: x: 4, y: 4, z: 8, core: 2. Of those that a mesh axis runs over, the one named last changes fastest.
Arguments:
- tokens: bfloat16 [32768, 2048], P(('dp', 'expert')), may hold values from -6 to 6
- norm_gain: bfloat16 [2048], replicated, may hold values from 0.099609375 to 1.8984375
- router_weight: bfloat16 [2048, 32], replicated, may hold values from -0.1875 to 0.1875
- w_gate: bfloat16 [32, 2048, 5120], P('expert', None, 'dp'), may hold values from -0.125 to 0.125
- w_up: bfloat16 [32, 2048, 5120], P('expert', None, 'dp'), may hold values from -0.125 to 0.125
- w_down: bfloat16 [32, 5120, 2048], P('expert', 'dp'), may hold values from -0.078125 to 0.078125
- selected: int32 [32, 1792], replicated, may hold values from 0 to 32767, as said below
Outputs:
- combined: bfloat16 [32768, 2048], P(('dp', 'expert'))
Inputs may be any that keep to these rules, and one draw needn't show every extreme that they name: `selected`: each row holds 1792 distinct token indices in ascending order. Of one row's indices at most 16 fall among one device's 128 tokens and at most 336 among the tokens of one index of dp; every row reaches both bounds.
All inputs are finite; a program needn't handle non-finite values.
Results may differ from a plain program's by a relative error of at most 0.0072.
Values may be sent and summed in bfloat16 or wider, within the bound.
A program may use at most 128 MiB of HBM per device.

v0:
```python
import jax
import jax.numpy as jnp
from jax import lax
from jax.sharding import PartitionSpec as P


def run_rank(labels):
    length = labels.shape[0]
    places = jnp.arange(length, dtype=jnp.int32)
    changes = jnp.concatenate([jnp.ones((1,), jnp.bool_), labels[1:] != labels[:-1]])
    starts = jnp.where(changes, places, 0)
    return places - lax.cummax(starts, axis=0)


def per_device(tokens, norm_gain, router_weight, w_gate, w_up, w_down, selected):
    dp_count = lax.axis_size("dp")
    expert_count = lax.axis_size("expert")
    tok_rows, model_width = tokens.shape
    experts, capacity = selected.shape
    peak_slots = 4 * tok_rows // experts
    dp_index = lax.axis_index("dp")
    expert_index = lax.axis_index("expert")
    source = dp_index * expert_count + expert_index
    activations = tokens.astype(jnp.float32)
    mean_square = jnp.mean(activations * activations, axis=1, keepdims=True)
    normed = (activations * lax.rsqrt(mean_square + 1e-06) * norm_gain.astype(jnp.float32)).astype(
        jnp.bfloat16
    )
    gate_probs = jax.nn.sigmoid(jnp.dot(normed, router_weight, preferred_element_type=jnp.float32))
    lowest = source * tok_rows
    below_count = jnp.sum((selected < lowest).astype(jnp.int32), axis=1)
    upto_count = jnp.sum((selected < lowest + tok_rows).astype(jnp.int32), axis=1)
    slot_range = jnp.arange(peak_slots, dtype=jnp.int32)
    places = jnp.clip(below_count[:, None] + slot_range[None, :], 0, capacity - 1)
    is_valid = slot_range[None, :] < (upto_count - below_count)[:, None]
    local_index = jnp.where(is_valid, jnp.take_along_axis(selected, places, axis=1) - lowest, 0)
    outgoing = jnp.where(is_valid[:, :, None], normed[local_index], 0)
    slot_gate = jnp.where(is_valid, jnp.take_along_axis(gate_probs.T, local_index, axis=1), 0.0)
    received = lax.all_to_all(outgoing, "expert", split_axis=0, concat_axis=0, tiled=True)
    expert_row = lax.dynamic_index_in_dim(selected, expert_index, 0, keepdims=False)
    owners = expert_row // tok_rows
    ranks = run_rank(owners)
    block_rows = expert_count * tok_rows
    row_room = 3 * capacity // (2 * dp_count)
    row_first = jnp.sum((expert_row < dp_index * block_rows).astype(jnp.int32))
    row_last = jnp.sum((expert_row < (dp_index + 1) * block_rows).astype(jnp.int32))
    wanted = row_first + jnp.arange(row_room, dtype=jnp.int32)
    is_usable = wanted < row_last
    clipped = jnp.clip(wanted, 0, capacity - 1)
    sender = owners[clipped] - dp_index * expert_count
    lookup = jnp.clip(sender * peak_slots + ranks[clipped], 0, expert_count * peak_slots - 1)
    packed = jnp.where(is_usable[:, None], received.reshape(-1, model_width)[lookup], 0)
    everything = lax.all_gather(packed, "dp", axis=0, tiled=True)
    row_owner = owners // expert_count
    row_index = row_owner * row_room + run_rank(row_owner)
    expert_rows = everything[row_index]
    gate_part = jnp.dot(expert_rows, w_gate[0], preferred_element_type=jnp.float32)
    up_part = jnp.dot(expert_rows, w_up[0], preferred_element_type=jnp.float32)
    hidden = (jax.nn.gelu(gate_part, approximate=True) * up_part).astype(jnp.bfloat16)
    partial_value = jnp.dot(hidden, w_down[0], preferred_element_type=jnp.float32)
    term_rows = (
        jnp.zeros((dp_count * row_room, model_width), jnp.float32).at[row_index].set(partial_value)
    )
    own_part = lax.psum_scatter(term_rows, "dp", scatter_dimension=0, tiled=True).astype(
        jnp.bfloat16
    )
    group_sources = dp_index * expert_count + jnp.arange(expert_count, dtype=jnp.int32)
    firsts = jnp.sum(
        (expert_row[None, :] < group_sources[:, None] * tok_rows).astype(jnp.int32), axis=1
    )
    lasts = jnp.sum(
        (expert_row[None, :] < (group_sources[:, None] + 1) * tok_rows).astype(jnp.int32), axis=1
    )
    offsets = jnp.clip(firsts[:, None] + slot_range[None, :] - row_first, 0, row_room - 1)
    fitting = slot_range[None, :] < (lasts - firsts)[:, None]
    returning = jnp.where(fitting[:, :, None], own_part[offsets], 0)
    arrived = lax.all_to_all(returning, "expert", split_axis=0, concat_axis=0, tiled=True)
    token_range = jnp.arange(tok_rows, dtype=jnp.int32)
    mixing = jnp.where(
        local_index.reshape(1, -1) == token_range[:, None], slot_gate.reshape(1, -1), 0.0
    )
    combined = jnp.dot(mixing, arrived.reshape(-1, model_width).astype(jnp.float32))
    return combined.astype(jnp.bfloat16)


def solution(mesh):
    in_specs = (
        P(("dp", "expert"), None),
        P(),
        P(),
        P("expert", None, "dp"),
        P("expert", None, "dp"),
        P("expert", "dp", None),
        P(),
    )
    out_specs = P(("dp", "expert"), None)
    return jax.shard_map(
        per_device, mesh=mesh, in_specs=in_specs, out_specs=out_specs, check_vma=False
    )
```

profile of v0, /device:TPU:8, one launch (start us, length us, event | category | flops | bytes accessed | tf_op | source)
XLA Modules:
  0.0 424.2 jit_solution(17303480411533940090)
XLA Ops:
  6.5 1.4 fusion.20
  10.0 4.5 %gather_fusion.6 = s32[512]{0:T(512)S(1)} fusion(s32[32,1792]{1,0:T(8,128)S(1)} %copy-done.1, s32[512]{0:T(512)S(1)} %reshape.666), kind=kCustom, calls=%fused_computation.6 | custom fusion | bytes 8192 | tf_op jit(solution)/shard_map/jit(take_along_axis)/gather | solution.py:36
  16.0 3.3 gather_fusion
  19.4 3.1 broadcast_select_fusion
  22.4 11.8 %all-to-all-start = ((bf16[32,16,2048]{2,1,0:T(8,128)(2,1)}), bf16[32,16,2048]{2,1,0:T(8,128)(2,1)}, u32[]{:S(2)}, u32[]{:S(2)}) async-start(bf16[32,16,2048]{2,1,0:T(8,128)(2,1)} %broadcast_select_fusion), calls=%async_computation | async-start | bytes 4194304 | tf_op jit(solution)/shard_map/all_to_all | solution.py:39
  35.6 2.5 gather_fusion.1
  39.0 2.5 gather_fusion.2
  42.9 38.8 %all-to-all-done = bf16[32,16,2048]{2,1,0:T(8,128)(2,1)} async-done(((bf16[32,16,2048]{2,1,0:T(8,128)(2,1)}), bf16[32,16,2048]{2,1,0:T(8,128)(2,1)}, u32[]{:S(2)}, u32[]{:S(2)}) %all-to-all-start) | async-done | bytes 2097184 | tf_op jit(solution)/shard_map/all_to_all | solution.py:39
  81.7 6.8 %gather_fusion.3 = bf16[336,2048]{1,0:T(8,128)(2,1)} fusion(bf16[512,2048]{1,0:T(8,128)(2,1)} %bitcast.4, s32[1024]{0:T(1024)S(1)} %pad_clamp_fusion.2), kind=kCustom, calls=%fused_computation.3 | custom fusion | bytes 2753856 | tf_op jit(solution)/shard_map/gather | solution.py:52
  88.6 2.6 broadcast_select_fusion.2
  91.9 62.4 %all-gather.2.cloned.1.call-done = bf16[2688,2048]{1,0:T(8,128)(2,1)} async-done(((bf16[336,2048]{1,0:T(8,128)(2,1)}), bf16[2688,2048]{1,0:T(8,128)(2,1)}) %all-gather.2.cloned.1.call-update) | async-done | bytes 11010064 | tf_op jit(solution)/shard_map/all_gather | solution.py:53
  154.4 20.3 %gather_fusion.4 = bf16[1792,2048]{1,0:T(8,128)(2,1)} fusion(bf16[2688,2048]{1,0:T(8,128)(2,1)} %all-gather.2.cloned.1.call-done, s32[2048]{0:T(1024)S(1)} %pad_clamp_fusion), kind=kCustom, calls=%fused_computation.4 | custom fusion | bytes 14687232 | tf_op jit(solution)/shard_map/gather | solution.py:56
  174.7 9.0 %fusion.14 = f32[1792,640]{1,0:T(8,128)S(1)} fusion(bf16[1792,2048]{1,0:T(8,128)(2,1)} %gather_fusion.4, bf16[1,2048,640]{2,1,0:T(8,128)(2,1)} %param.10), kind=kOutput, calls=%fused_computation.24 | convolution fusion | flops 4697620480 | bytes 14548992 | tf_op jit(solution)/shard_map/dot_general | solution.py:57
  183.7 6.6 %fusion.10 = bf16[1792,640]{1,0:T(8,128)(2,1)S(1)} fusion(f32[1792,640]{1,0:T(8,128)S(1)} %fusion.14, bf16[1792,2048]{1,0:T(8,128)(2,1)S(1)} %copy-done.2, bf16[1,2048,640]{2,1,0:T(8,128)(2,1)S(1)} %copy-done.4), kind=kOutput, calls=%fused_computation.20 | convolution fusion | flops 4709089280 | bytes 16842752 | tf_op jit(solution)/shard_map/dot_general | solution.py:58
  190.3 9.2 %fusion.11 = f32[1792,2048]{1,0:T(8,128)} fusion(bf16[1792,640]{1,0:T(8,128)(2,1)S(1)} %fusion.10, bf16[1,640,2048]{2,1,0:T(8,128)(2,1)S(1)} %copy-done), kind=kOutput, calls=%fused_computation.21 | convolution fusion | flops 4697620480 | bytes 19595264 | tf_op jit(solution)/shard_map/dot_general | solution.py:60
  199.5 25.0 %scatter_custom_fusion = f32[2688,2048]{1,0:T(8,128)} fusion(s32[1792]{0:T(1024)S(1)} %fusion.38, f32[1792,2048]{1,0:T(8,128)} %fusion.11, f32[]{:T(128)} %constant.100.clone.1), kind=kCustom, calls=%fused_computation.9 | custom fusion | bytes 22020608 | tf_op jit(solution)/shard_map/scatter | solution.py:62
  225.7 118.5 %reduce-scatter.2.cloned.1.call-done = f32[336,2048]{1,0:T(8,128)} async-done(((f32[2688,2048]{1,0:T(8,128)}), f32[336,2048]{1,0:T(8,128)}) %reduce-scatter.2.cloned.1.call-update) | async-done | bytes 2752528 | tf_op jit(solution)/shard_map/reduce_scatter | solution.py:64
  344.1 3.1 convert_element_type.52
  347.2 6.8 %gather_fusion.5 = bf16[512,2048]{1,0:T(8,128)(2,1)} fusion(bf16[336,2048]{1,0:T(8,128)(2,1)} %convert_element_type.52, s32[1024]{0:T(1024)S(1)} %pad_clamp_fusion.1), kind=kCustom, calls=%fused_computation.5 | custom fusion | bytes 4196352 | tf_op jit(solution)/shard_map/gather | solution.py:76
  354.0 3.1 broadcast_select_fusion.1
  357.1 10.3 %all-to-all-start.1 = ((bf16[32,16,2048]{2,1,0:T(8,128)(2,1)}), bf16[32,16,2048]{2,1,0:T(8,128)(2,1)}, u32[]{:S(2)}, u32[]{:S(2)}) async-start(bf16[32,16,2048]{2,1,0:T(8,128)(2,1)} %broadcast_select_fusion.1), calls=%async_computation.2 | async-start | bytes 4194304 | tf_op jit(solution)/shard_map/all_to_all | solution.py:77
  368.5 4.7 %gather_fusion.7 = bf16[512]{0:T(512)(128)(2,1)S(1)} fusion(bf16[32,128]{1,0:T(8,128)(2,1)S(1)} %fusion.19, s32[512]{0:T(512)S(1)} %reshape.672), kind=kCustom, calls=%fused_computation.7 | custom fusion | bytes 6144 | tf_op jit(solution)/shard_map/jit(take_along_axis)/gather | solution.py:38
  373.2 41.3 %all-to-all-done.1 = bf16[32,16,2048]{2,1,0:T(8,128)(2,1)} async-done(((bf16[32,16,2048]{2,1,0:T(8,128)(2,1)}), bf16[32,16,2048]{2,1,0:T(8,128)(2,1)}, u32[]{:S(2)}, u32[]{:S(2)}) %all-to-all-start.1) | async-done | bytes 2097184 | tf_op jit(solution)/shard_map/all_to_all | solution.py:77
  414.5 2.8 convolution_convert_fusion
  (70 shorter events, 10.0 us)
Async XLA Ops:
  6.5 183.8 %copy-start = (bf16[1,640,2048]{2,1,0:T(8,128)(2,1)S(1)}, bf16[1,640,2048]{2,1,0:T(8,128)(2,1)}, u32[]{:S(2)}) copy-start(bf16[1,640,2048]{2,1,0:T(8,128)(2,1)} %param.12) | copy-start | bytes 7864324
  6.5 3.4 copy-start.1
  22.4 59.3 %all-to-all-start = ((bf16[32,16,2048]{2,1,0:T(8,128)(2,1)}), bf16[32,16,2048]{2,1,0:T(8,128)(2,1)}, u32[]{:S(2)}, u32[]{:S(2)}) async-start(bf16[32,16,2048]{2,1,0:T(8,128)(2,1)} %broadcast_select_fusion), calls=%async_computation | async-start | bytes 4194304 | tf_op jit(solution)/shard_map/all_to_all | solution.py:39
  34.2 120.2 %all-gather.2.cloned.1.call-start = ((), (), s32[]{:S(2)}) async-start(), calls=%async_computation.3 | async-start | bytes 12386304 | tf_op jit(solution)/shard_map/all_gather | solution.py:53
  91.2 252.9 %reduce-scatter.2.cloned.1.call-start = ((), (), s32[]{:S(2)}) async-start(), calls=%async_computation.4 | async-start | bytes 24772608 | tf_op jit(solution)/shard_map/reduce_scatter | solution.py:64
  174.7 9.0 %copy-start.2 = (bf16[1792,2048]{1,0:T(8,128)(2,1)S(1)}, bf16[1792,2048]{1,0:T(8,128)(2,1)}, u32[]{:S(2)}) copy-start(bf16[1792,2048]{1,0:T(8,128)(2,1)} %gather_fusion.4) | copy-start | bytes 22020100
  174.7 9.0 %copy-start.4 = (bf16[1,2048,640]{2,1,0:T(8,128)(2,1)S(1)}, bf16[1,2048,640]{2,1,0:T(8,128)(2,1)}, u32[]{:S(2)}) copy-start(bf16[1,2048,640]{2,1,0:T(8,128)(2,1)} %param.11) | copy-start | bytes 7864324
  357.1 11.1 %copy-start.3 = (bf16[2048,32]{0,1:T(8,128)(2,1)S(1)}, bf16[2048,32]{0,1:T(8,128)(2,1)}, u32[]{:S(2)}) copy-start(bf16[2048,32]{0,1:T(8,128)(2,1)} %param.9) | copy-start | bytes 393220
  357.1 57.4 %all-to-all-start.1 = ((bf16[32,16,2048]{2,1,0:T(8,128)(2,1)}), bf16[32,16,2048]{2,1,0:T(8,128)(2,1)}, u32[]{:S(2)}, u32[]{:S(2)}) async-start(bf16[32,16,2048]{2,1,0:T(8,128)(2,1)} %broadcast_select_fusion.1), calls=%async_computation.2 | async-start | bytes 4194304 | tf_op jit(solution)/shard_map/all_to_all | solution.py:77
Sparse Core Ops, SparseCore 0:
  91.3 63.0 all-gather.1
  224.7 119.4 reduce-scatter.1
where the time goes:
time: 427 us; the launch traced here: 424 us
  waiting for transfers between devices  261 us (61%)
  local copies, waits for them, and re-layouts  78 us (18%)
  matrix products  27.9 us (7%)
  starting transfers between devices  22.2 us (5%)
  other arithmetic  21.3 us (5%)
  between operations  13.7 us (3%)
    reduce_scatter x1, waiting for transfers between devices, per_device(): lax.psum_scatter(term_rows, 'dp', scatter_dimension=0, tiled=True)  118 us
    all_gather x1, waiting for transfers between devices, per_device(): everything = lax.all_gather(packed, 'dp', axis=0, tiled=True)  62.4 us
    all_to_all x1, waiting for transfers between devices, per_device(): lax.all_to_all(returning, 'expert', split_axis=0, concat_axis=0, tiled=True)  41.3 us
    all_to_all x1, waiting for transfers between devices, per_device(): lax.all_to_all(outgoing, 'expert', split_axis=0, concat_axis=0, tiled=True)  38.8 us
    scatter x1, local copies, waits for them, and re-layouts, per_device(): jnp.zeros((dp_count * row_room, model_width), jnp.float32).at[row_index]  25 us
    gather x1, local copies, waits for them, and re-layouts, per_device(): expert_rows = everything[row_index]  20.3 us
    all_to_all x1, starting transfers between devices, per_device(): lax.all_to_all(outgoing, 'expert', split_axis=0, concat_axis=0, tiled=True)  11.8 us
    all_to_all x1, starting transfers between devices, per_device(): lax.all_to_all(returning, 'expert', split_axis=0, concat_axis=0, tiled=True)  10.3 us
  transfers between devices with their start and end apart: 4, of which 4 were waited for; matrix products, arithmetic and copies ran while one was open for 4% of the time, Pallas kernels for 0%

commit v1 on v0

v1 whole, which is shorter than its diff:
```python
import functools

import jax
import jax.numpy as jnp
from jax import lax
from jax.experimental import pallas as pl
from jax.experimental.pallas import tpu as pltpu
from jax.sharding import PartitionSpec as P

SLOT = 16
ROOM = 336
HALF = 176
CHUNKS = 8


def copy_pairs(mesh_id):
    return functools.partial(pltpu.make_async_remote_copy, device_id_type=mesh_id)


def moe_kernel(
    n_expert,
    s_ref,
    n_ref,
    p_ref,
    q_ref,
    mh_ref,
    ml_ref,
    wg_ref,
    wu_ref,
    wd_ref,
    o_ref,
    outg,
    recv,
    gath,
    acc,
    hid,
    wgu,
    wdn,
    prec,
    hrec,
    srec,
    arr,
    wsem,
    a_s,
    a_r,
    g_s,
    g_r,
    r_s,
    r_r,
    b_s,
    b_r,
):
    nc = CHUNKS
    width = outg.shape[2]
    ff = hid.shape[2]
    rows = n_expert * SLOT
    remote = copy_pairs(pl.DeviceIdType.MESH)
    d = lax.axis_index("dp")
    e = lax.axis_index("expert")
    x, core = d // 2, d % 2
    xr, xl, xo = (x + 1) % 4, (x + 3) % 4, (x + 2) % 4
    dl, dr, do, dq = xl * 2 + core, xr * 2 + core, xo * 2 + core, x * 2 + (1 - core)
    right, left, partner = (dr, e), (dl, e), (dq, e)

    def peer(k):
        return (d, (e + k) % n_expert)

    loads = [
        pltpu.make_async_copy(wg_ref, wgu.at[:, pl.ds(0, ff)], wsem.at[0]),
        pltpu.make_async_copy(wu_ref, wgu.at[:, pl.ds(ff, ff)], wsem.at[1]),
        pltpu.make_async_copy(wd_ref, wdn, wsem.at[2]),
    ]
    for load in loads:
        load.start()

    barrier = pltpu.get_barrier_semaphore()

    def greet(k, carry):
        pl.semaphore_signal(barrier, inc=1, device_id=peer(k), device_id_type=pl.DeviceIdType.MESH)
        return carry

    lax.fori_loop(1, n_expert, greet, 0)
    for who in (right, left, partner):
        pl.semaphore_signal(barrier, inc=1, device_id=who, device_id_type=pl.DeviceIdType.MESH)

    def lanes(c):
        return pl.ds(pl.multiple_of(c * width, width), width)

    def fill(c, carry):
        outg[c] = jnp.dot(
            s_ref[...], n_ref[:, lanes(c)], preferred_element_type=jnp.float32
        ).astype(jnp.bfloat16)
        return carry

    lax.fori_loop(0, nc, fill, 0)
    acc[...] = jnp.zeros_like(acc)
    pl.semaphore_wait(barrier, n_expert - 1 + 3)

    def slot(k):
        return pl.ds(pl.multiple_of(k * SLOT, SLOT), SLOT)

    def scatter(src, dst, send, got):
        def chunk(c, carry):
            def one(k, carry):
                to = (e + k) % n_expert
                remote(
                    src_ref=src.at[c, slot(to)],
                    dst_ref=dst.at[c, slot(e)],
                    send_sem=send.at[c],
                    recv_sem=got.at[c],
                    device_id=(d, to),
                ).start()
                return carry

            lax.fori_loop(1, n_expert, one, 0)
            pltpu.make_async_copy(src.at[c, slot(e)], dst.at[c, slot(e)], got.at[c]).start()
            return carry

        return chunk

    def all_got(dst, got, c):
        pltpu.make_async_copy(dst.at[c], dst.at[c], got.at[c]).wait()

    def all_sent(src, send, c):
        part = src.at[c, pl.ds(0, rows - SLOT)]
        pltpu.make_async_copy(part, part, send.at[c]).wait()

    lax.fori_loop(0, nc, scatter(outg, recv, a_s, a_r), 0)

    lo, hi = pl.ds(0, HALF), pl.ds(HALF, ROOM - HALF)

    def gcopy(c, j):
        block, to = [
            (gath.at[c, d], right),
            (gath.at[c, d], left),
            (gath.at[c, d], partner),
            (gath.at[c, dl, lo], right),
            (gath.at[c, dr, hi], left),
            (gath.at[c, dl], partner),
            (gath.at[c, dr], partner),
            (gath.at[c, do], partner),
        ][j]
        return remote(
            src_ref=block,
            dst_ref=block,
            send_sem=g_s.at[c, j],
            recv_sem=g_r.at[c, j],
            device_id=to,
        )

    def up(c, b):
        total = acc[b] + jnp.dot(
            gath[c, b],
            wgu[pl.ds(pl.multiple_of(c * width, width), width), :],
            preferred_element_type=jnp.float32,
        )

        @pl.when(c < nc - 1)
        def _():
            acc[b] = total

        @pl.when(c == nc - 1)
        def _():
            v, u = total[:, :ff], total[:, ff:]
            act = 0.5 * v * (1.0 + jnp.tanh(0.7978845608028654 * (v + 0.044715 * (v * v * v))))
            hid[b] = (act * u).astype(jnp.bfloat16)

    for load in loads:
        load.wait()

    def several(c, blocks):
        def step(i, carry):
            b = blocks[-1]
            for n in range(len(blocks) - 2, -1, -1):
                b = jnp.where(i == n, blocks[n], b)
            up(c, b)
            return carry

        lax.fori_loop(0, len(blocks), step, 0)

    def dispatch(i, carry):
        @pl.when(i < nc)
        def _():
            c = i
            all_got(recv, a_r, c)
            gath[c, d] = jnp.dot(
                p_ref[...], recv[c], preferred_element_type=jnp.float32
            ).astype(jnp.bfloat16)
            for j in (0, 1, 2):
                gcopy(c, j).start()

        @pl.when((i >= 1) & (i < nc + 1))
        def _():
            c = i - 1
            gcopy(c, 0).wait_recv()
            gcopy(c, 3).start()
            gcopy(c, 1).wait_recv()
            gcopy(c, 4).start()
            gcopy(c, 5).start()
            gcopy(c, 6).start()
            gcopy(c, 2).wait_recv()
            several(c, (d, dl, dr, dq))

        @pl.when((i >= 2) & (i < nc + 2))
        def _():
            c = i - 2
            gcopy(c, 3).wait_recv()
            gcopy(c, 4).wait_recv()
            gcopy(c, 7).start()
            gcopy(c, 5).wait_recv()
            gcopy(c, 6).wait_recv()
            several(c, (do, xl * 2 + (1 - core), xr * 2 + (1 - core)))
            gcopy(c, 7).wait_recv()
            several(c, (xo * 2 + (1 - core),))

        return carry

    lax.fori_loop(0, nc + 2, dispatch, 0)

    def drain(c, carry):
        for j in range(8):
            gcopy(c, j).wait_send()
        all_sent(outg, a_s, c)
        return carry

    lax.fori_loop(0, nc, drain, 0)

    def mine(c, k):
        return acc.at[k + 4 * (c % 2), :, pl.ds(pl.multiple_of((c // 2) * width, width), width)]

    def rcopy(c, j):
        src, dst, to = [
            (gath.at[c, 0], prec.at[c, 0], partner),
            (gath.at[c, 1], prec.at[c, 1], partner),
            (gath.at[c, 2], prec.at[c, 2], partner),
            (gath.at[c, 3], prec.at[c, 3], partner),
            (gath.at[c, 4, lo], hrec.at[c, lo], right),
            (gath.at[c, 4, hi], hrec.at[c, hi], left),
            (gath.at[c, 5], srec.at[c, 0], right),
            (gath.at[c, 6], srec.at[c, 1], left),
        ][j]
        return remote(
            src_ref=src, dst_ref=dst, send_sem=r_s.at[c, j], recv_sem=r_r.at[c, j], device_id=to
        )

    def down(c, b):
        return jnp.dot(hid[b], wdn[:, lanes(c)], preferred_element_type=jnp.float32)

    def pair(c, k):
        return mine(c, k)[...] + prec[c, k].astype(jnp.float32)

    def combine(i, carry):
        @pl.when(i < nc)
        def _():
            c = i

            for k in range(4):
                gath[c, k] = down(c, k * 2 + (1 - core)).astype(jnp.bfloat16)
                rcopy(c, k).start()

            def keep(k, carry):
                mine(c, k)[...] = down(c, k * 2 + core)
                return carry

            lax.fori_loop(0, 4, keep, 0)

        @pl.when((i >= 1) & (i < nc + 1))
        def _():
            c = i - 1
            for k in range(4):
                rcopy(c, k).wait_recv()
            gath[c, 4] = pair(c, xo).astype(jnp.bfloat16)
            rcopy(c, 4).start()
            rcopy(c, 5).start()

        @pl.when((i >= 2) & (i < nc + 2))
        def _():
            c = i - 2
            to_right, to_left = pair(c, xr), pair(c, xl)
            rcopy(c, 4).wait_recv()
            gath[c, 5, lo] = (to_right[:HALF] + hrec[c, lo].astype(jnp.float32)).astype(jnp.bfloat16)
            gath[c, 5, hi] = to_right[HALF:].astype(jnp.bfloat16)
            rcopy(c, 6).start()
            rcopy(c, 5).wait_recv()
            gath[c, 6, lo] = to_left[:HALF].astype(jnp.bfloat16)
            gath[c, 6, hi] = (to_left[HALF:] + hrec[c, hi].astype(jnp.float32)).astype(jnp.bfloat16)
            rcopy(c, 7).start()

        @pl.when(i >= 3)
        def _():
            c = i - 3
            total = pair(c, x)
            rcopy(c, 6).wait_recv()
            rcopy(c, 7).wait_recv()
            total = total + srec[c, 0].astype(jnp.float32) + srec[c, 1].astype(jnp.float32)
            outg[c] = jnp.dot(
                q_ref[...], total.astype(jnp.bfloat16), preferred_element_type=jnp.float32
            ).astype(jnp.bfloat16)
            scatter(outg, arr, b_s, b_r)(c, 0)

        return carry

    lax.fori_loop(0, nc + 3, combine, 0)

    def finish(c, carry):
        all_got(arr, b_r, c)
        got = arr[c]
        o_ref[:, lanes(c)] = (
            jnp.dot(mh_ref[...], got, preferred_element_type=jnp.float32)
            + jnp.dot(ml_ref[...], got, preferred_element_type=jnp.float32)
        ).astype(jnp.bfloat16)
        return carry

    lax.fori_loop(0, nc, finish, 0)

    def drain_back(c, carry):
        for j in range(8):
            rcopy(c, j).wait_send()
        all_sent(outg, b_s, c)
        return carry

    lax.fori_loop(0, nc, drain_back, 0)


def per_device(tokens, norm_gain, router_weight, w_gate, w_up, w_down, selected):
    n_dp = lax.axis_size("dp")
    n_expert = lax.axis_size("expert")
    tok_rows, model_width = tokens.shape
    experts, capacity = selected.shape
    ff = w_gate.shape[2]
    width = model_width // CHUNKS
    rows = n_expert * SLOT
    d = lax.axis_index("dp")
    e = lax.axis_index("expert")
    activations = tokens.astype(jnp.float32)
    mean_square = jnp.mean(activations * activations, axis=1, keepdims=True)
    normed = (activations * lax.rsqrt(mean_square + 1e-06) * norm_gain.astype(jnp.float32)).astype(
        jnp.bfloat16
    )
    gate_probs = jax.nn.sigmoid(jnp.dot(normed, router_weight, preferred_element_type=jnp.float32))

    lowest = (d * n_expert + e) * tok_rows
    below = jnp.sum((selected < lowest).astype(jnp.int32), axis=1, keepdims=True)
    inside = (selected >= lowest) & (selected < lowest + tok_rows)
    rank = jnp.arange(capacity, dtype=jnp.int32)[None, :] - below
    slots = jnp.arange(SLOT, dtype=jnp.int32)
    local = jnp.sum(
        jnp.where(
            inside[:, None, :] & (rank[:, None, :] == slots[None, :, None]),
            selected[:, None, :] - lowest + 1,
            0,
        ),
        axis=2,
    )
    token_range = jnp.arange(1, tok_rows + 1, dtype=jnp.int32)
    flat = local.reshape(rows)
    take = (flat[:, None] == token_range[None, :]).astype(jnp.bfloat16)
    mix = jnp.where(
        token_range[:, None, None] == local[None, :, :], gate_probs[:, :, None], 0.0
    ).reshape(tok_rows, rows)
    mix_high = lax.reduce_precision(mix, 8, 7)
    mix_low = (mix - mix_high).astype(jnp.bfloat16)
    mix_high = mix_high.astype(jnp.bfloat16)

    expert_row = lax.dynamic_index_in_dim(selected, e, 0, keepdims=False)
    bounds = (d * n_expert + jnp.arange(n_expert + 1, dtype=jnp.int32)) * tok_rows
    counts = jnp.sum((expert_row[None, :] < bounds[:, None]).astype(jnp.int32), axis=1)
    first, last = counts[:-1], counts[1:]
    place = first[:, None] - counts[0] + slots[None, :]
    place = jnp.where(slots[None, :] < (last - first)[:, None], place, -1).reshape(rows)
    room = jnp.arange(ROOM, dtype=jnp.int32)
    pack = (room[:, None] == place[None, :]).astype(jnp.bfloat16)
    unpack = (place[:, None] == room[None, :]).astype(jnp.bfloat16)

    vmem = pl.BlockSpec(memory_space=pltpu.VMEM)
    hbm = pl.BlockSpec(memory_space=pl.ANY)
    bf16, f32 = jnp.bfloat16, jnp.float32
    dma = pltpu.SemaphoreType.DMA
    return pl.pallas_call(
        functools.partial(moe_kernel, n_expert),
        out_shape=jax.ShapeDtypeStruct((tok_rows, model_width), bf16),
        in_specs=[vmem] * 6 + [hbm] * 3,
        out_specs=vmem,
        scratch_shapes=[
            pltpu.VMEM((CHUNKS, rows, width), bf16),
            pltpu.VMEM((CHUNKS, rows, width), bf16),
            pltpu.VMEM((CHUNKS, n_dp, ROOM, width), bf16),
            pltpu.VMEM((n_dp, ROOM, 2 * ff), f32),
            pltpu.VMEM((n_dp, ROOM, ff), bf16),
            pltpu.VMEM((model_width, 2 * ff), bf16),
            pltpu.VMEM((ff, model_width), bf16),
            pltpu.VMEM((CHUNKS, n_dp // 2, ROOM, width), bf16),
            pltpu.VMEM((CHUNKS, ROOM, width), bf16),
            pltpu.VMEM((CHUNKS, 2, ROOM, width), bf16),
            pltpu.VMEM((CHUNKS, rows, width), bf16),
            dma((3,)),
            dma((CHUNKS,)),
            dma((CHUNKS,)),
            dma((CHUNKS, 8)),
            dma((CHUNKS, 8)),
            dma((CHUNKS, 8)),
            dma((CHUNKS, 8)),
            dma((CHUNKS,)),
            dma((CHUNKS,)),
        ],
        compiler_params=pltpu.CompilerParams(
            collective_id=0, has_side_effects=True, vmem_limit_bytes=67043328
        ),
    )(
        take,
        normed,
        pack,
        unpack,
        mix_high,
        mix_low,
        w_gate.reshape(model_width, ff),
        w_up.reshape(model_width, ff),
        w_down.reshape(ff, model_width),
    )


def solution(mesh):
    in_specs = (
        P(("dp", "expert"), None),
        P(),
        P(),
        P("expert", None, "dp"),
        P("expert", None, "dp"),
        P("expert", "dp", None),
        P(),
    )
    out_specs = P(("dp", "expert"), None)
    return jax.shard_map(
        per_device, mesh=mesh, in_specs=in_specs, out_specs=out_specs, check_vma=False
    )
```

time: 427 us -> 159 us (0.37)
  waiting for transfers between devices: 261 us -> 0 us
  Pallas kernels: 0 us -> 145 us
  local copies, waits for them, and re-layouts: 78 us -> 3.84 us
  matrix products: 27.9 us -> 0.29 us
  starting transfers between devices: 22.2 us -> 0 us
  between operations: 13.7 us -> 0.08 us
  other arithmetic: 21.3 us -> 9.22 us
    pallas_call x0 -> x1, Pallas kernels: none -> 145 us  [per_device(): pl.pallas_call(functools.partial(moe_kernel, n_expert), out_shape=jax.Sha...]
    reduce_scatter x1 -> x0, waiting for transfers between devices: 118 us -> none  [per_device(): lax.psum_scatter(term_rows, 'dp', scatter_dimension=0, tiled=True)]
    all_to_all x2 -> x0, waiting for transfers between devices: 80.2 us -> none  [the longest x1 41.3 us: per_device(): lax.all_to_all(returning, 'expert', split_axis=0, concat_axis=0, tiled=True)]
    all_gather x1 -> x0, waiting for transfers between devices: 62.4 us -> none  [per_device(): everything = lax.all_gather(packed, 'dp', axis=0, tiled=True)]
    gather x11 -> x0, local copies, waits for them, and re-layouts: 51.8 us -> none  [the longest x1 20.3 us: per_device(): expert_rows = everything[row_index]]
    dot_general x4 -> x0, matrix products: 27.6 us -> none  [the longest x1 9.19 us: per_device(): jnp.dot(hidden, w_down[0], preferred_element_type=jnp.float32)]
    scatter x1 -> x0, local copies, waits for them, and re-layouts: 25 us -> none  [per_device(): jnp.zeros((dp_count * row_room, model_width), jnp.float32).at[row_index]]
    all_to_all x2 -> x0, starting transfers between devices: 22.1 us -> none  [the longest x1 11.8 us: per_device(): lax.all_to_all(outgoing, 'expert', split_axis=0, concat_axis=0, tiled=True)]
  transfers between devices with their start and end apart: 4 -> 0, of which waited for: 4 -> 0; matrix products, arithmetic and copies ran while one was open for 4% -> 0% of each run, Pallas kernels for 0% -> 0%
where the time goes in v1:
time: 159 us; the launch traced here: 158 us
  Pallas kernels  145 us (91%)
  other arithmetic  9.22 us (6%)
  local copies, waits for them, and re-layouts  3.84 us (2%)
    pallas_call x1, Pallas kernels, per_device(): pl.pallas_call(functools.partial(moe_kernel, n_expert), out_shape=jax.Sha...  145 us

profile of v1, /device:TPU:8, one launch (start us, length us, event | category | flops | bytes accessed | tf_op | source)
XLA Modules:
  0.0 158.5 jit_solution(10543187029504658367)
XLA Ops:
  0.0 1.3 fusion.4
  1.3 0.9 dynamic-slice_reduce_fusion
  2.2 0.2 convert_reduce_fusion
  2.4 0.1 slice_subtract_fusion
  2.5 0.7 convert_element_type.33
  3.2 0.1 add_select_fusion
  3.3 0.1 select_n.31
  3.3 1.0 compare_and_fusion
  4.3 1.1 convert_reduce_fusion.1
  5.4 0.1 iota_subtract_fusion
  5.5 1.1 select_reduce_fusion
  6.7 0.1 eq.71
  6.7 0.8 compare_convert_fusion.s_ref
  7.5 0.8 fusion.8.p_ref
  8.3 0.9 fusion.7.q_ref
  9.2 0.2 fusion.6.n_ref
  9.4 0.0 copy-start
  9.4 0.8 copy-done
  10.2 0.0 copy-done.2
  10.2 0.3 fusion.3
  10.6 0.1 copy.10
  10.7 0.8 fusion.9
  11.5 145.1 %shard_map.73 = bf16[128,2048]{1,0:T(8,128)(2,1)} custom-call(bf16[512,128]{1,0:T(8,128)(2,1)} %compare_convert_fusion.s_ref, bf16[128,2048]{1,0:T(8,128)(2,1)} %copy-done, bf16[336,512]{1,0:T(8,128)(2,1)} %fusion.8.p_ref, bf16[512,336]{1,0:T(8,128)(2,1)} %fusion.7.q_ref, bf16[128,512]{1,0:T(8,128)(2,1)} %get-tuple-element.6.mh_ref, ...), custom_call_target="tpu_custom_call" | custom-call | tf_op jit(solution)/shard_map/pallas_call | solution.py:379
  156.6 1.9 %copy.12 = bf16[128,2048]{1,0:T(8,128)(2,1)} copy(bf16[128,2048]{1,0:T(8,128)(2,1)} %shard_map.73) | data formatting | bytes 1048576
  (7 shorter events, 0.0 us)
Async XLA Ops:
  0.0 9.2 %copy-start.1 = (bf16[128,2048]{1,0:T(8,128)(2,1)S(1)}, bf16[128,2048]{1,0:T(8,128)(2,1)}, u32[]{:S(2)}) copy-start(bf16[128,2048]{1,0:T(8,128)(2,1)} %param.7) | copy-start | bytes 1572868
  0.0 10.2 %copy-start.2 = (bf16[2048,32]{0,1:T(8,128)(2,1)S(1)}, bf16[2048,32]{0,1:T(8,128)(2,1)}, u32[]{:S(2)}) copy-start(bf16[2048,32]{0,1:T(8,128)(2,1)} %param.9) | copy-start | bytes 393220
  9.4 0.8 copy-start

commit v2 on v1

--- a/solution.py
+++ b/solution.py
@@ -19,12 +19,10 @@
 
 def moe_kernel(
     n_expert,
-    s_ref,
-    n_ref,
-    p_ref,
-    q_ref,
-    mh_ref,
-    ml_ref,
+    tok_ref,
+    gain_ref,
+    rw_ref,
+    sel_ref,
     wg_ref,
     wu_ref,
     wd_ref,
@@ -40,6 +38,13 @@
     hrec,
     srec,
     arr,
+    s_ref,
+    n_ref,
+    p_ref,
+    q_ref,
+    m_ref,
+    lg_ref,
+    gt_ref,
     wsem,
     a_s,
     a_r,
@@ -65,6 +70,19 @@
     def peer(k):
         return (d, (e + k) % n_expert)
 
+    barrier = pltpu.get_barrier_semaphore()
+
+    def greet(k, carry):
+        pl.semaphore_signal(barrier, inc=1, device_id=peer(k), device_id_type=pl.DeviceIdType.MESH)
+        return carry
+
+    lax.fori_loop(1, n_expert, greet, 0)
+    for who in (right, left, partner):
+        pl.semaphore_signal(barrier, inc=1, device_id=who, device_id_type=pl.DeviceIdType.MESH)
+
+    def lanes(c):
+        return pl.ds(pl.multiple_of(c * width, width), width)
+
     loads = [
         pltpu.make_async_copy(wg_ref, wgu.at[:, pl.ds(0, ff)], wsem.at[0]),
         pltpu.make_async_copy(wu_ref, wgu.at[:, pl.ds(ff, ff)], wsem.at[1]),
@@ -73,27 +91,41 @@
     for load in loads:
         load.start()
 
-    barrier = pltpu.get_barrier_semaphore()
-
-    def greet(k, carry):
-        pl.semaphore_signal(barrier, inc=1, device_id=peer(k), device_id_type=pl.DeviceIdType.MESH)
-        return carry
-
-    lax.fori_loop(1, n_expert, greet, 0)
-    for who in (right, left, partner):
-        pl.semaphore_signal(barrier, inc=1, device_id=who, device_id_type=pl.DeviceIdType.MESH)
-
-    def lanes(c):
-        return pl.ds(pl.multiple_of(c * width, width), width)
-
-    def fill(c, carry):
-        outg[c] = jnp.dot(
-            s_ref[...], n_ref[:, lanes(c)], preferred_element_type=jnp.float32
-        ).astype(jnp.bfloat16)
-        return carry
-
-    lax.fori_loop(0, nc, fill, 0)
-    acc[...] = jnp.zeros_like(acc)
+    f32, bf16 = jnp.float32, jnp.bfloat16
+    tok_rows = tok_ref.shape[0]
+    experts, capacity = sel_ref.shape
+
+    def iota(shape, axis):
+        return lax.broadcasted_iota(jnp.int32, shape, axis)
+
+    def one_hot(mask):
+        return jnp.where(mask, 1.0, 0.0).astype(bf16)
+
+    def flip(a):
+        n = a.shape[1]
+        eye = one_hot(iota((n, n), 0) == iota((n, n), 1))
+        turned = lax.dot_general(eye, a, (((1,), (1,)), ((), ())), preferred_element_type=f32)
+        return turned.astype(bf16)
+
+    tok = tok_ref[...].astype(f32)
+    mean_square = jnp.mean(tok * tok, axis=1, keepdims=True)
+    n_ref[...] = (tok * lax.rsqrt(mean_square + 1e-06) * gain_ref[...].astype(f32)).astype(bf16)
+
+    lowest = (d * n_expert + e) * tok_rows
+    sel = sel_ref[...]
+    below = jnp.sum(jnp.where(sel < lowest, 1.0, 0.0), axis=1, keepdims=True)
+    rank = iota((experts, capacity), 1).astype(f32) - below
+    inside = (sel >= lowest) & (sel < lowest + tok_rows)
+    local = jnp.where(inside, sel - lowest + 1, 0).astype(f32)
+    token = iota((experts, tok_rows), 1).astype(f32) + 1.0
+    by_slot = []
+    for k in range(SLOT):
+        found = jnp.sum(jnp.where(rank == float(k), local, 0.0), axis=1, keepdims=True)
+        by_slot.append(jnp.where(found == token, 1.0, 0.0))
+    by_slot = jnp.concatenate(by_slot, axis=0).astype(bf16)
+    r = iota((rows, rows), 0)
+    order = one_hot(iota((rows, rows), 1) == (r & (SLOT - 1)) * experts + lax.shift_right_logical(r, 4))
+    s_ref[...] = jnp.dot(order, by_slot, preferred_element_type=f32).astype(bf16)
     pl.semaphore_wait(barrier, n_expert - 1 + 3)
 
     def slot(k):
@@ -125,7 +157,25 @@
         part = src.at[c, pl.ds(0, rows - SLOT)]
         pltpu.make_async_copy(part, part, send.at[c]).wait()
 
-    lax.fori_loop(0, nc, scatter(outg, recv, a_s, a_r), 0)
+    def fill(c, carry):
+        outg[c] = jnp.dot(s_ref[...], n_ref[:, lanes(c)], preferred_element_type=f32).astype(bf16)
+        return scatter(outg, recv, a_s, a_r)(c, carry)
+
+    lax.fori_loop(0, nc, fill, 0)
+
+    row = sel_ref[pl.ds(e, 1), :]
+    slot_row = iota((rows, 1), 0)
+    lower = (d * n_expert + lax.shift_right_logical(slot_row, 4)) * tok_rows
+    rank_in = (slot_row & (SLOT - 1)).astype(f32)
+    first = jnp.sum(jnp.where(row < lower, 1.0, 0.0), axis=1, keepdims=True)
+    last = jnp.sum(jnp.where(row < lower + tok_rows, 1.0, 0.0), axis=1, keepdims=True)
+    start = jnp.sum(jnp.where(row < d * (n_expert * tok_rows), 1.0, 0.0), axis=1, keepdims=True)
+    place = jnp.where(rank_in < last - first, first - start + rank_in, -1.0)
+    q_ref[...] = one_hot(place == iota((rows, ROOM), 1).astype(f32))
+    p_ref[...] = flip(q_ref[...])
+    m_ref[...] = flip(s_ref[...])
+    acc[...] = jnp.zeros_like(acc)
+    lg_ref[...] = jnp.zeros_like(lg_ref)
 
     lo, hi = pl.ds(0, HALF), pl.ds(HALF, ROOM - HALF)
 
@@ -183,11 +233,15 @@
         def _():
             c = i
             all_got(recv, a_r, c)
-            gath[c, d] = jnp.dot(
-                p_ref[...], recv[c], preferred_element_type=jnp.float32
-            ).astype(jnp.bfloat16)
+            packed = jnp.dot(p_ref[...], recv[c], preferred_element_type=f32).astype(bf16)
+            gath[c, d] = packed
             for j in (0, 1, 2):
                 gcopy(c, j).start()
+            lg_ref[...] += jnp.dot(
+                packed,
+                rw_ref[pl.ds(pl.multiple_of(c * width, width), width), :],
+                preferred_element_type=f32,
+            )
 
         @pl.when((i >= 1) & (i < nc + 1))
         def _():
@@ -224,6 +278,10 @@
         return carry
 
     lax.fori_loop(0, nc, drain, 0)
+
+    own_logit = jnp.where(iota((ROOM, experts), 1) == e, lg_ref[...], 0.0)
+    gate = jax.nn.sigmoid(jnp.sum(own_logit, axis=1, keepdims=True))
+    gt_ref[...] = jnp.broadcast_to(gate, gt_ref.shape)
 
     def mine(c, k):
         return acc.at[k + 4 * (c % 2), :, pl.ds(pl.multiple_of((c // 2) * width, width), width)]
@@ -293,6 +351,7 @@
             rcopy(c, 6).wait_recv()
             rcopy(c, 7).wait_recv()
             total = total + srec[c, 0].astype(jnp.float32) + srec[c, 1].astype(jnp.float32)
+            total = total * gt_ref[...]
             outg[c] = jnp.dot(
                 q_ref[...], total.astype(jnp.bfloat16), preferred_element_type=jnp.float32
             ).astype(jnp.bfloat16)
@@ -305,10 +364,7 @@
     def finish(c, carry):
         all_got(arr, b_r, c)
         got = arr[c]
-        o_ref[:, lanes(c)] = (
-            jnp.dot(mh_ref[...], got, preferred_element_type=jnp.float32)
-            + jnp.dot(ml_ref[...], got, preferred_element_type=jnp.float32)
-        ).astype(jnp.bfloat16)
+        o_ref[:, lanes(c)] = jnp.dot(m_ref[...], got, preferred_element_type=f32).astype(bf16)
         return carry
 
     lax.fori_loop(0, nc, finish, 0)
@@ -330,48 +386,6 @@
     ff = w_gate.shape[2]
     width = model_width // CHUNKS
     rows = n_expert * SLOT
-    d = lax.axis_index("dp")
-    e = lax.axis_index("expert")
-    activations = tokens.astype(jnp.float32)
-    mean_square = jnp.mean(activations * activations, axis=1, keepdims=True)
-    normed = (activations * lax.rsqrt(mean_square + 1e-06) * norm_gain.astype(jnp.float32)).astype(
-        jnp.bfloat16
-    )
-    gate_probs = jax.nn.sigmoid(jnp.dot(normed, router_weight, preferred_element_type=jnp.float32))
-
-    lowest = (d * n_expert + e) * tok_rows
-    below = jnp.sum((selected < lowest).astype(jnp.int32), axis=1, keepdims=True)
-    inside = (selected >= lowest) & (selected < lowest + tok_rows)
-    rank = jnp.arange(capacity, dtype=jnp.int32)[None, :] - below
-    slots = jnp.arange(SLOT, dtype=jnp.int32)
-    local = jnp.sum(
-        jnp.where(
-            inside[:, None, :] & (rank[:, None, :] == slots[None, :, None]),
-            selected[:, None, :] - lowest + 1,
-            0,
-        ),
-        axis=2,
-    )
-    token_range = jnp.arange(1, tok_rows + 1, dtype=jnp.int32)
-    flat = local.reshape(rows)
-    take = (flat[:, None] == token_range[None, :]).astype(jnp.bfloat16)
-    mix = jnp.where(
-        token_range[:, None, None] == local[None, :, :], gate_probs[:, :, None], 0.0
-    ).reshape(tok_rows, rows)
-    mix_high = lax.reduce_precision(mix, 8, 7)
-    mix_low = (mix - mix_high).astype(jnp.bfloat16)
-    mix_high = mix_high.astype(jnp.bfloat16)
-
-    expert_row = lax.dynamic_index_in_dim(selected, e, 0, keepdims=False)
-    bounds = (d * n_expert + jnp.arange(n_expert + 1, dtype=jnp.int32)) * tok_rows
-    counts = jnp.sum((expert_row[None, :] < bounds[:, None]).astype(jnp.int32), axis=1)
-    first, last = counts[:-1], counts[1:]
-    place = first[:, None] - counts[0] + slots[None, :]
-    place = jnp.where(slots[None, :] < (last - first)[:, None], place, -1).reshape(rows)
-    room = jnp.arange(ROOM, dtype=jnp.int32)
-    pack = (room[:, None] == place[None, :]).astype(jnp.bfloat16)
-    unpack = (place[:, None] == room[None, :]).astype(jnp.bfloat16)
-
     vmem = pl.BlockSpec(memory_space=pltpu.VMEM)
     hbm = pl.BlockSpec(memory_space=pl.ANY)
     bf16, f32 = jnp.bfloat16, jnp.float32
@@ -379,7 +393,7 @@
     return pl.pallas_call(
         functools.partial(moe_kernel, n_expert),
         out_shape=jax.ShapeDtypeStruct((tok_rows, model_width), bf16),
-        in_specs=[vmem] * 6 + [hbm] * 3,
+        in_specs=[vmem] * 4 + [hbm] * 3,
         out_specs=vmem,
         scratch_shapes=[
             pltpu.VMEM((CHUNKS, rows, width), bf16),
@@ -393,6 +407,13 @@
             pltpu.VMEM((CHUNKS, ROOM, width), bf16),
             pltpu.VMEM((CHUNKS, 2, ROOM, width), bf16),
             pltpu.VMEM((CHUNKS, rows, width), bf16),
+            pltpu.VMEM((rows, tok_rows), bf16),
+            pltpu.VMEM((tok_rows, model_width), bf16),
+            pltpu.VMEM((ROOM, rows), bf16),
+            pltpu.VMEM((rows, ROOM), bf16),
+            pltpu.VMEM((tok_rows, rows), bf16),
+            pltpu.VMEM((ROOM, experts), f32),
+            pltpu.VMEM((ROOM, width), f32),
             dma((3,)),
             dma((CHUNKS,)),
             dma((CHUNKS,)),
@@ -407,12 +428,10 @@
             collective_id=0, has_side_effects=True, vmem_limit_bytes=67043328
         ),
     )(
-        take,
-        normed,
-        pack,
-        unpack,
-        mix_high,
-        mix_low,
+        tokens,
+        norm_gain.reshape(1, model_width),
+        router_weight,
+        selected,
         w_gate.reshape(model_width, ff),
         w_up.reshape(model_width, ff),
         w_down.reshape(ff, model_width),

time: 159 us -> 151 us (0.950)
  other arithmetic: 9.22 us -> 0 us
    convert_element_type x6 -> x0, other arithmetic: 4.21 us -> none  [the longest x1 0.89 us: per_device(): unpack = (place[:, None] == room[None, :]).astype(jnp.bfloat16)]
    reduce_sum x4 -> x0, other arithmetic: 3.72 us -> none  [the longest x1 1.29 us: per_device(): mean_square = jnp.mean(activations * activations, axis=1, keepdims=True)]
    unnamed x7 -> x2, local copies, waits for them, and re-layouts: 2.68 us -> 3.79 us
where the time goes in v2:
time: 151 us
  Pallas kernels  146 us (97%)
  local copies, waits for them, and re-layouts  5.07 us (3%)
    pallas_call x1, Pallas kernels, per_device(): pl.pallas_call(functools.partial(moe_kernel, n_expert), out_shape=jax.Sha...  146 us
    unnamed x2, local copies, waits for them, and re-layouts  3.79 us

profile of v2, /device:TPU:8, one launch (start us, length us, event | category | flops | bytes accessed | tf_op | source)
XLA Modules:
  0.0 150.6 jit_solution(9358238384933738021)
XLA Ops:
  0.0 1.3 reshape.12.gain_ref
  1.3 1.9 %copy.8.rw_ref = bf16[2048,32]{1,0:T(8,128)(2,1)} copy(bf16[2048,32]{0,1:T(8,128)(2,1)} %param.9) | data formatting | bytes 262144 | tf_op args[2]
  3.2 145.6 %shard_map.73 = bf16[128,2048]{1,0:T(8,128)(2,1)} custom-call(bf16[128,2048]{1,0:T(8,128)(2,1)} %tok_ref.1, bf16[1,2048]{1,0:T(2,128)(2,1)} %reshape.12.gain_ref, bf16[2048,32]{1,0:T(8,128)(2,1)} %copy.8.rw_ref, s32[32,1792]{1,0:T(8,128)} %sel_ref.1, bf16[2048,640]{1,0:T(8,128)(2,1)} %bitcast.3, bf16[2048,640]{1,0:T(8,128)(2,1)} %bitcast.4, ...), custom_call_target="tpu_custom_call" | custom-call | tf_op jit(solution)/shard_map/pallas_call | solution.py:393
  148.8 1.9 %copy.10 = bf16[128,2048]{1,0:T(8,128)(2,1)} copy(bf16[128,2048]{1,0:T(8,128)(2,1)} %shard_map.73) | data formatting | bytes 1048576

commit v3 on v2

--- a/solution.py
+++ b/solution.py
@@ -109,7 +109,7 @@
 
     tok = tok_ref[...].astype(f32)
     mean_square = jnp.mean(tok * tok, axis=1, keepdims=True)
-    n_ref[...] = (tok * lax.rsqrt(mean_square + 1e-06) * gain_ref[...].astype(f32)).astype(bf16)
+    n_ref[...] = (tok * lax.rsqrt(mean_square + 1e-06) * gain_ref[...].astype(f32)[None, :]).astype(bf16)
 
     lowest = (d * n_expert + e) * tok_rows
     sel = sel_ref[...]
@@ -198,22 +198,23 @@
             device_id=to,
         )
 
+    def act(v, u):
+        g = 0.5 * v * (1.0 + jnp.tanh(0.7978845608028654 * (v + 0.044715 * (v * v * v))))
+        return (g * u).astype(bf16)
+
     def up(c, b):
-        total = acc[b] + jnp.dot(
-            gath[c, b],
-            wgu[pl.ds(pl.multiple_of(c * width, width), width), :],
-            preferred_element_type=jnp.float32,
-        )
-
-        @pl.when(c < nc - 1)
-        def _():
-            acc[b] = total
+        @pl.when((c % 2 == 1) & (c < nc - 1))
+        def _():
+            a = jnp.concatenate([gath[c - 1, b], gath[c, b]], axis=1)
+            w = pl.ds(pl.multiple_of((c - 1) * width, 2 * width), 2 * width)
+            acc[b] += jnp.dot(a, wgu[w, :], preferred_element_type=f32)
 
         @pl.when(c == nc - 1)
         def _():
-            v, u = total[:, :ff], total[:, ff:]
-            act = 0.5 * v * (1.0 + jnp.tanh(0.7978845608028654 * (v + 0.044715 * (v * v * v))))
-            hid[b] = (act * u).astype(jnp.bfloat16)
+            a = jnp.concatenate([gath[c - 1, b], gath[c, b]], axis=1)
+            w = pl.ds(pl.multiple_of((c - 1) * width, 2 * width), 2 * width)
+            total = acc[b] + jnp.dot(a, wgu[w, :], preferred_element_type=f32)
+            hid[b] = act(total[:, :ff], total[:, ff:])
 
     for load in loads:
         load.wait()
@@ -237,10 +238,8 @@
             gath[c, d] = packed
             for j in (0, 1, 2):
                 gcopy(c, j).start()
-            lg_ref[...] += jnp.dot(
-                packed,
-                rw_ref[pl.ds(pl.multiple_of(c * width, width), width), :],
-                preferred_element_type=f32,
+            lg_ref[...] += lax.dot_general(
+                packed, rw_ref[:, lanes(c)], (((1,), (1,)), ((), ())), preferred_element_type=f32
             )
 
         @pl.when((i >= 1) & (i < nc + 1))
@@ -304,37 +303,24 @@
     def down(c, b):
         return jnp.dot(hid[b], wdn[:, lanes(c)], preferred_element_type=jnp.float32)
 
-    def pair(c, k):
-        return mine(c, k)[...] + prec[c, k].astype(jnp.float32)
+    def pair(c, k, n):
+        return mine(c, k)[...] + prec[c, n].astype(jnp.float32)
 
     def combine(i, carry):
-        @pl.when(i < nc)
-        def _():
-            c = i
-
-            for k in range(4):
-                gath[c, k] = down(c, k * 2 + (1 - core)).astype(jnp.bfloat16)
-                rcopy(c, k).start()
-
-            def keep(k, carry):
-                mine(c, k)[...] = down(c, k * 2 + core)
-                return carry
-
-            lax.fori_loop(0, 4, keep, 0)
-
         @pl.when((i >= 1) & (i < nc + 1))
         def _():
             c = i - 1
-            for k in range(4):
-                rcopy(c, k).wait_recv()
-            gath[c, 4] = pair(c, xo).astype(jnp.bfloat16)
+            rcopy(c, 0).wait_recv()
+            gath[c, 4] = pair(c, xo, 0).astype(jnp.bfloat16)
             rcopy(c, 4).start()
             rcopy(c, 5).start()
 
         @pl.when((i >= 2) & (i < nc + 2))
         def _():
             c = i - 2
-            to_right, to_left = pair(c, xr), pair(c, xl)
+            rcopy(c, 1).wait_recv()
+            rcopy(c, 2).wait_recv()
+            to_right, to_left = pair(c, xr, 1), pair(c, xl, 2)
             rcopy(c, 4).wait_recv()
             gath[c, 5, lo] = (to_right[:HALF] + hrec[c, lo].astype(jnp.float32)).astype(jnp.bfloat16)
             gath[c, 5, hi] = to_right[HALF:].astype(jnp.bfloat16)
@@ -344,10 +330,26 @@
             gath[c, 6, hi] = (to_left[HALF:] + hrec[c, hi].astype(jnp.float32)).astype(jnp.bfloat16)
             rcopy(c, 7).start()
 
+        @pl.when(i < nc)
+        def _():
+            c = i
+
+            for k in range(4):
+                k_x = (xo, xr, xl, x)[k]
+                gath[c, k] = down(c, k_x * 2 + (1 - core)).astype(jnp.bfloat16)
+                rcopy(c, k).start()
+
+            def keep(k, carry):
+                mine(c, k)[...] = down(c, k * 2 + core)
+                return carry
+
+            lax.fori_loop(0, 4, keep, 0)
+
         @pl.when(i >= 3)
         def _():
             c = i - 3
-            total = pair(c, x)
+            rcopy(c, 3).wait_recv()
+            total = pair(c, x, 3)
             rcopy(c, 6).wait_recv()
             rcopy(c, 7).wait_recv()
             total = total + srec[c, 0].astype(jnp.float32) + srec[c, 1].astype(jnp.float32)
@@ -429,8 +431,8 @@
         ),
     )(
         tokens,
-        norm_gain.reshape(1, model_width),
-        router_weight,
+        norm_gain,
+        router_weight.T,
         selected,
         w_gate.reshape(model_width, ff),
         w_up.reshape(model_width, ff),

time: 151 us -> 143 us (0.947)
  Pallas kernels: 146 us -> 140 us
  local copies, waits for them, and re-layouts: 5.07 us -> 1.88 us
    pallas_call x1, Pallas kernels: 146 us -> 140 us  [per_device(): pl.pallas_call(functools.partial(moe_kernel, n_expert), out_shape=jax.Sha...]
    unnamed x2 -> x1, local copies, waits for them, and re-layouts: 3.79 us -> 1.88 us
where the time goes in v3:
time: 143 us; the launch traced here: 142 us
  Pallas kernels  140 us (98%)
  local copies, waits for them, and re-layouts  1.88 us (1%)
    pallas_call x1, Pallas kernels, per_device(): pl.pallas_call(functools.partial(moe_kernel, n_expert), out_shape=jax.Sha...  140 us

profile of v3, /device:TPU:8, one launch (start us, length us, event | category | flops | bytes accessed | tf_op | source)
XLA Modules:
  0.0 142.0 jit_solution(6931708604621311990)
XLA Ops:
  0.0 140.1 %shard_map.73 = bf16[128,2048]{1,0:T(8,128)(2,1)} custom-call(bf16[128,2048]{1,0:T(8,128)(2,1)} %tok_ref.1, bf16[2048]{0:T(1024)(128)(2,1)} %gain_ref.1, bf16[32,2048]{1,0:T(8,128)(2,1)} %bitcast.7, s32[32,1792]{1,0:T(8,128)} %sel_ref.1, bf16[2048,640]{1,0:T(8,128)(2,1)} %bitcast.4, bf16[2048,640]{1,0:T(8,128)(2,1)} %bitcast.5, bf16[640,2048]{1,0:T(8,128)(2,1)} %bitcast.6), custom_call_target="tpu_custom_call" | custom-call | tf_op jit(solution)/shard_map/pallas_call | solution.py:395
  140.1 1.9 %copy.9 = bf16[128,2048]{1,0:T(8,128)(2,1)} copy(bf16[128,2048]{1,0:T(8,128)(2,1)} %shard_map.73) | data formatting | bytes 1048576

commit v4 on v3

--- a/solution.py
+++ b/solution.py
@@ -203,17 +203,21 @@
         return (g * u).astype(bf16)
 
     def up(c, b):
-        @pl.when((c % 2 == 1) & (c < nc - 1))
+        @pl.when((c % 2 == 1) & (c < nc - 2))
         def _():
             a = jnp.concatenate([gath[c - 1, b], gath[c, b]], axis=1)
             w = pl.ds(pl.multiple_of((c - 1) * width, 2 * width), 2 * width)
             acc[b] += jnp.dot(a, wgu[w, :], preferred_element_type=f32)
 
+        @pl.when(c == nc - 2)
+        def _():
+            w = pl.ds((nc - 2) * width, width)
+            acc[b] += jnp.dot(gath[c, b], wgu[w, :], preferred_element_type=f32)
+
         @pl.when(c == nc - 1)
         def _():
-            a = jnp.concatenate([gath[c - 1, b], gath[c, b]], axis=1)
-            w = pl.ds(pl.multiple_of((c - 1) * width, 2 * width), 2 * width)
-            total = acc[b] + jnp.dot(a, wgu[w, :], preferred_element_type=f32)
+            w = pl.ds((nc - 1) * width, width)
+            total = acc[b] + jnp.dot(gath[c, b], wgu[w, :], preferred_element_type=f32)
             hid[b] = act(total[:, :ff], total[:, ff:])
 
     for load in loads:
@@ -330,21 +334,6 @@
             gath[c, 6, hi] = (to_left[HALF:] + hrec[c, hi].astype(jnp.float32)).astype(jnp.bfloat16)
             rcopy(c, 7).start()
 
-        @pl.when(i < nc)
-        def _():
-            c = i
-
-            for k in range(4):
-                k_x = (xo, xr, xl, x)[k]
-                gath[c, k] = down(c, k_x * 2 + (1 - core)).astype(jnp.bfloat16)
-                rcopy(c, k).start()
-
-            def keep(k, carry):
-                mine(c, k)[...] = down(c, k * 2 + core)
-                return carry
-
-            lax.fori_loop(0, 4, keep, 0)
-
         @pl.when(i >= 3)
         def _():
             c = i - 3
@@ -358,6 +347,21 @@
                 q_ref[...], total.astype(jnp.bfloat16), preferred_element_type=jnp.float32
             ).astype(jnp.bfloat16)
             scatter(outg, arr, b_s, b_r)(c, 0)
+
+        @pl.when(i < nc)
+        def _():
+            c = i
+
+            for k in range(4):
+                k_x = (xo, xr, xl, x)[k]
+                gath[c, k] = down(c, k_x * 2 + (1 - core)).astype(jnp.bfloat16)
+                rcopy(c, k).start()
+
+            def keep(k, carry):
+                mine(c, k)[...] = down(c, k * 2 + core)
+                return carry
+
+            lax.fori_loop(0, 4, keep, 0)
 
         return carry
 

time: 143 us -> 142 us (level)
  no operation moved by 1% of the time
where the time goes in v4:
time: 142 us
  Pallas kernels  140 us (99%)
  local copies, waits for them, and re-layouts  1.88 us (1%)
    pallas_call x1, Pallas kernels, per_device(): pl.pallas_call(functools.partial(moe_kernel, n_expert), out_shape=jax.Sha...  140 us

profile of v4, /device:TPU:8, one launch (start us, length us, event | category | flops | bytes accessed | tf_op | source)
XLA Modules:
  0.0 142.2 jit_solution(8546989755232962912)
XLA Ops:
  0.0 140.3 %shard_map.73 = bf16[128,2048]{1,0:T(8,128)(2,1)} custom-call(bf16[128,2048]{1,0:T(8,128)(2,1)} %tok_ref.1, bf16[2048]{0:T(1024)(128)(2,1)} %gain_ref.1, bf16[32,2048]{1,0:T(8,128)(2,1)} %bitcast.7, s32[32,1792]{1,0:T(8,128)} %sel_ref.1, bf16[2048,640]{1,0:T(8,128)(2,1)} %bitcast.4, bf16[2048,640]{1,0:T(8,128)(2,1)} %bitcast.5, bf16[640,2048]{1,0:T(8,128)(2,1)} %bitcast.6), custom_call_target="tpu_custom_call" | custom-call | tf_op jit(solution)/shard_map/pallas_call | solution.py:399
  140.4 1.9 %copy.9 = bf16[128,2048]{1,0:T(8,128)(2,1)} copy(bf16[128,2048]{1,0:T(8,128)(2,1)} %shard_map.73) | data formatting | bytes 1048576
